TPU v7x, 32 devices: a whole 2x2x4 slice. The times are simulated.
32 devices in a mesh: cluster: 8 (over z, x), sub: 4 (over y, core).
Axes of the slice: x: 2, y: 2, z: 4, core: 2. Of those that a mesh axis runs over, the one named last changes fastest.
Arguments:
- mantissas: int32 [8, 64, 168, 128], P('cluster', 'sub'), may hold values from -128 to 127
- exponents: int32 [8, 64, 14], P('cluster', 'sub'), may hold values from -9 to -6
- channel: bfloat16 [8, 64, 2, 64, 128], P('cluster', 'sub'), may hold values from -0.5 to 0.5
- inverses: bfloat16 [8, 64, 2, 128, 128], P('cluster', 'sub'), may hold values from -4 to 4, as said below
Outputs:
- detected: bfloat16 [64, 168, 256], P('sub')
Inputs may be any that keep to these rules, and one draw needn't show every extreme that they name: `inverses`: each real part has a positive diagonal; the matrices are otherwise dense.
All inputs are finite; a program needn't handle non-finite values.
Results may differ from a plain program's by a relative error of at most 0.0074.
Values may be sent and summed in bfloat16 or wider, within the bound.
A program may use at most 64 MiB of HBM per device.

v0:
```python
import jax
import jax.numpy as jnp
from jax import lax
from jax.sharding import PartitionSpec as P

ITERS = 3
RHO = 0.5


def complex_block(real, imag):
    top = jnp.concatenate([real, -imag], axis=-1)
    bottom = jnp.concatenate([imag, real], axis=-1)
    return jnp.concatenate([top, bottom], axis=-2)


def per_device(mantissas, exponents, channel, inverses):
    clusters = lax.axis_size("cluster")
    mant = mantissas[0]
    blocks, vectors, _ = mant.shape
    expo = exponents[0]
    scale = jnp.repeat(jnp.exp2(expo.astype(jnp.float32)), vectors // expo.shape[1], axis=1)
    signal = (mant.astype(jnp.float32) * scale[:, :, None]).astype(jnp.bfloat16)
    match = complex_block(channel[0, :, 0], channel[0, :, 1])
    matched_filter = jnp.einsum("rsa,rau->rsu", signal, match, preferred_element_type=jnp.float32)
    solve_block = complex_block(inverses[0, :, 0], inverses[0, :, 1])
    width = matched_filter.shape[2]
    consensus = jnp.zeros(matched_filter.shape, jnp.float32)
    dual = jnp.zeros(matched_filter.shape, jnp.float32)
    for step in range(ITERS):
        rhs = (matched_filter + RHO * (consensus - dual)).astype(jnp.bfloat16)
        local = jnp.einsum("rsk,rjk->rsj", rhs, solve_block, preferred_element_type=jnp.float32)
        term = local + dual
        flat = term.reshape(blocks * vectors, width)
        share = lax.psum_scatter(flat, "cluster", scatter_dimension=0, tiled=True)
        average = (share / clusters).astype(jnp.bfloat16)
        gathered = lax.all_gather(average, "cluster", axis=0, tiled=True)
        consensus = gathered.reshape(blocks, vectors, width).astype(jnp.float32)
        dual = term - consensus
    users = width // 2
    column_list = jnp.sum(consensus * consensus, axis=(0, 1))
    partial_value = column_list[:users] + column_list[users:]
    total_power = lax.psum(partial_value, "sub")
    power = total_power / (blocks * lax.axis_size("sub") * vectors)
    factor = lax.rsqrt(power + 1e-06)
    factor = jnp.concatenate([factor, factor])
    return (consensus * factor).astype(jnp.bfloat16)


def solution(mesh):
    placed = (
        P("cluster", "sub", None, None),
        P("cluster", "sub", None),
        P("cluster", "sub", None, None, None),
        P("cluster", "sub", None, None, None),
    )
    return jax.shard_map(
        per_device, mesh=mesh, in_specs=placed, out_specs=P("sub", None, None), check_vma=False
    )
```

profile of v0, /device:TPU:0, one launch (start us, length us, event | category | flops | bytes accessed | tf_op | source)
XLA Modules:
  0.0 393.4 jit_solution(11023630587310864629)
XLA Ops:
  6.5 0.0 copy-start
  6.5 0.0 copy-start.4
  6.5 0.0 reduce-scatter.4.cloned.1.call-start
  6.5 1.1 fusion.28
  7.6 1.1 slice_bitcast_fusion.2
  8.7 1.9 fusion.29
  10.6 0.0 copy-done
  10.6 1.1 slice_bitcast_fusion
  11.7 0.0 copy-done.4
  11.7 0.1 copy.15
  11.8 0.1 broadcast_in_dim.4
  11.9 0.1 mul.28
  12.0 0.0 copy-start.2
  12.0 0.0 copy-start.3
  12.0 2.0 fusion.15
  14.0 0.0 copy-done.2
  14.0 0.0 copy-done.3
  14.1 3.5 fusion.13
  17.6 0.0 copy-start.1
  17.6 0.0 reduce-scatter.4.cloned.1.call-update
  17.6 0.0 all-gather.4.cloned.1.call-start
  17.6 74.6 %reduce-scatter.4.cloned.1.call-done = f32[336,256]{1,0:T(8,128)} async-done(((f32[2688,256]{1,0:T(8,128)}), f32[336,256]{1,0:T(8,128)}) %reduce-scatter.4.cloned.1.call-update) | async-done | bytes 344080 | tf_op jit(solution)/shard_map/reduce_scatter | solution.py:34
  92.2 1.7 multiply_convert_fusion.3
  93.9 0.0 all-gather.4.cloned.1.call-update
  93.9 0.0 reduce-scatter.6.cloned.1.call-start
  94.0 41.8 %all-gather.4.cloned.1.call-done = bf16[2688,256]{1,0:T(8,128)(2,1)} async-done(((bf16[336,256]{1,0:T(8,128)(2,1)}), bf16[2688,256]{1,0:T(8,128)(2,1)}) %all-gather.4.cloned.1.call-update) | async-done | bytes 1376272 | tf_op jit(solution)/shard_map/all_gather | solution.py:36
  135.7 0.0 copy-done.1
  135.8 6.5 %fusion.6 = f32[16,168,256]{2,1,0:T(8,128)} fusion(f32[16,168,256]{2,1,0:T(8,128)} %fusion.13, bf16[16,168,256]{2,1,0:T(8,128)(2,1)} %bitcast.41, f32[16,168,256]{2,1,0:T(8,128)S(1)} %fusion.15, bf16[16,128,128]{2,1,0:T(8,128)(2,1)} %get-tuple-element.6, bf16[16,128,128]{2,1,0:T(8,128)(2,1)} %get-tuple-element.5, bf16[16,128,128]{2,1,0:T(8,128)(2,1)S(1)} %copy-done.1), kind=kOutput, calls=%fused_computation.12 | convolution fusion | flops 366903296 | bytes 11206656 | tf_op jit(solution)/shard_map/rsk,rjk->rsj/dot_general | solution.py:31
  142.2 0.0 reduce-scatter.6.cloned.1.call-update
  142.2 0.0 all-gather.6.cloned.1.call-start
  142.3 70.3 %reduce-scatter.6.cloned.1.call-done = f32[336,256]{1,0:T(8,128)} async-done(((f32[2688,256]{1,0:T(8,128)}), f32[336,256]{1,0:T(8,128)}) %reduce-scatter.6.cloned.1.call-update) | async-done | bytes 344080 | tf_op jit(solution)/shard_map/reduce_scatter | solution.py:34
  212.6 1.7 multiply_convert_fusion.2
  214.3 0.0 all-gather.6.cloned.1.call-update
  214.3 0.0 reduce-scatter.8.cloned.1.call-start
  214.4 41.6 %all-gather.6.cloned.1.call-done = bf16[2688,256]{1,0:T(8,128)(2,1)} async-done(((bf16[336,256]{1,0:T(8,128)(2,1)}), bf16[2688,256]{1,0:T(8,128)(2,1)}) %all-gather.6.cloned.1.call-update) | async-done | bytes 1376272 | tf_op jit(solution)/shard_map/all_gather | solution.py:36
  256.0 6.4 %fusion.7 = f32[16,168,256]{2,1,0:T(8,128)} fusion(f32[16,168,256]{2,1,0:T(8,128)} %fusion.6, bf16[16,168,256]{2,1,0:T(8,128)(2,1)} %bitcast.40, f32[16,168,256]{2,1,0:T(8,128)S(1)} %fusion.15, bf16[16,128,128]{2,1,0:T(8,128)(2,1)} %get-tuple-element.6, bf16[16,128,128]{2,1,0:T(8,128)(2,1)} %get-tuple-element.5, bf16[16,128,128]{2,1,0:T(8,128)(2,1)S(1)} %copy-done.1), kind=kOutput, calls=%fused_computation.13 | convolution fusion | flops 366903296 | bytes 11206656 | tf_op jit(solution)/shard_map/rsk,rjk->rsj/dot_general | solution.py:31
  262.4 0.0 reduce-scatter.8.cloned.1.call-update
  262.4 0.0 all-gather.8.cloned.1.call-start
  262.4 70.7 %reduce-scatter.8.cloned.1.call-done = f32[336,256]{1,0:T(8,128)} async-done(((f32[2688,256]{1,0:T(8,128)}), f32[336,256]{1,0:T(8,128)}) %reduce-scatter.8.cloned.1.call-update) | async-done | bytes 344080 | tf_op jit(solution)/shard_map/reduce_scatter | solution.py:34
  333.2 1.7 multiply_convert_fusion.1
  334.9 0.0 all-gather.8.cloned.1.call-update
  334.9 41.6 %all-gather.8.cloned.1.call-done = bf16[2688,256]{1,0:T(8,128)(2,1)} async-done(((bf16[336,256]{1,0:T(8,128)(2,1)}), bf16[2688,256]{1,0:T(8,128)(2,1)}) %all-gather.8.cloned.1.call-update) | async-done | bytes 1376272 | tf_op jit(solution)/shard_map/all_gather | solution.py:36
  376.5 1.7 multiply_reduce_fusion
  378.2 5.7 %psum.7 = f32[128]{0:T(128)S(1)} all-reduce(f32[128]{0:T(128)S(1)} %slice_add_fusion), channel_id=1, replica_groups=mesh['cluster'=8,'sub'=4] {'sub'}, use_global_device_ids=true, to_apply=%region_4.0 | all-reduce | flops 128 | bytes 1024 | tf_op jit(solution)/shard_map/psum | solution.py:42
  383.9 2.7 multiply_convert_fusion
  (4 shorter events, 0.0 us)
Async XLA Ops:
  6.5 4.1 %copy-start = (bf16[1,16,2,128,128]{4,3,2,1,0:T(8,128)(2,1)S(1)}, bf16[1,16,2,128,128]{4,3,2,1,0:T(8,128)(2,1)}, u32[]{:S(2)}) copy-start(bf16[1,16,2,128,128]{4,3,2,1,0:T(8,128)(2,1)} %param.7) | copy-start | bytes 3145732
  6.5 5.2 %copy-start.4 = (s32[1,16,14]{1,0,2:T(1,128)S(1)}, s32[1,16,14]{1,0,2:T(1,128)}, u32[]{:S(2)}) copy-start(s32[1,16,14]{1,0,2:T(1,128)} %param.5) | copy-start | bytes 2692
  6.5 85.7 %reduce-scatter.4.cloned.1.call-start = ((), (), s32[]{:S(2)}) async-start(), calls=%async_computation.3 | async-start | bytes 3096576 | tf_op jit(solution)/shard_map/reduce_scatter | solution.py:34
  12.0 2.0 copy-start.2
  12.0 2.0 copy-start.3
  17.6 118.2 %copy-start.1 = (bf16[16,128,128]{2,1,0:T(8,128)(2,1)S(1)}, bf16[16,128,128]{2,1,0:T(8,128)(2,1)}, u32[]{:S(2)}) copy-start(bf16[16,128,128]{2,1,0:T(8,128)(2,1)} %fusion.29) | copy-start | bytes 1572868
  17.6 118.2 %all-gather.4.cloned.1.call-start = ((), (), s32[]{:S(2)}) async-start(), calls=%async_computation.4 | async-start | bytes 1548288 | tf_op jit(solution)/shard_map/all_gather | solution.py:36
  93.9 118.7 %reduce-scatter.6.cloned.1.call-start = ((), (), s32[]{:S(2)}) async-start(), calls=%async_computation.5 | async-start | bytes 3096576 | tf_op jit(solution)/shard_map/reduce_scatter | solution.py:34
  142.2 113.7 %all-gather.6.cloned.1.call-start = ((), (), s32[]{:S(2)}) async-start(), calls=%async_computation.6 | async-start | bytes 1548288 | tf_op jit(solution)/shard_map/all_gather | solution.py:36
  214.3 118.9 %reduce-scatter.8.cloned.1.call-start = ((), (), s32[]{:S(2)}) async-start(), calls=%async_computation.7 | async-start | bytes 3096576 | tf_op jit(solution)/shard_map/reduce_scatter | solution.py:34
  262.4 114.1 %all-gather.8.cloned.1.call-start = ((), (), s32[]{:S(2)}) async-start(), calls=%async_computation.8 | async-start | bytes 1548288 | tf_op jit(solution)/shard_map/all_gather | solution.py:36
Sparse Core Ops, SparseCore 0:
  17.7 74.4 reduce-scatter.3
  94.4 41.2 all-gather.3
  142.4 70.2 reduce-scatter.5
  214.7 41.2 all-gather.5
  262.5 70.6 reduce-scatter.7
  335.2 41.2 all-gather.7
where the time goes:
time: 394 us; the launch traced here: 393 us
  waiting for transfers between devices  341 us (87%)
  matrix products  18.4 us (5%)
  between operations  13.5 us (3%)
  other arithmetic  12.4 us (3%)
  blocking collectives  5.66 us (1%)
    reduce_scatter x3, waiting for transfers between devices, per_device(): share = lax.psum_scatter(flat, 'cluster', scatter_dimension=0, tiled=True)  216 us
    all_gather x3, waiting for transfers between devices, per_device(): gathered = lax.all_gather(average, 'cluster', axis=0, tiled=True)  125 us
    dot_general x3, matrix products, per_device(): jnp.einsum('rsk,rjk->rsj', rhs, solve_block, preferred_element_type=jnp.f...  16.4 us
  transfers between devices with their start and end apart: 6, of which 6 were waited for; matrix products, arithmetic and copies ran while one was open for 0% of the time, Pallas kernels for 0%

commit v1 on v0

--- a/solution.py
+++ b/solution.py
@@ -33,7 +33,16 @@
         flat = term.reshape(blocks * vectors, width)
         share = lax.psum_scatter(flat, "cluster", scatter_dimension=0, tiled=True)
         average = (share / clusters).astype(jnp.bfloat16)
-        gathered = lax.all_gather(average, "cluster", axis=0, tiled=True)
+        ring = [average]
+        for hop in range(7):
+            ring.append(
+                lax.ppermute(ring[-1], "cluster", [(dev, (dev + 1) % 8) for dev in range(8)])
+            )
+        gathered = jnp.roll(
+            jnp.concatenate(ring[::-1], axis=0),
+            (lax.axis_index("cluster") + 1) * ring[0].shape[0],
+            axis=0,
+        )
         consensus = gathered.reshape(blocks, vectors, width).astype(jnp.float32)
         dual = term - consensus
     users = width // 2

time: 394 us -> 450 us (1.14)
  waiting for transfers between devices: 341 us -> 390 us
  matrix products: 18.4 us -> 8.77 us
  local copies, waits for them, and re-layouts: 2.45 us -> 9.52 us
  other arithmetic: 12.4 us -> 19.4 us
    ppermute x0 -> x21, waiting for transfers between devices: none -> 177 us  [per_device(): lax.ppermute(ring[-1], 'cluster', [(dev, (dev + 1) % 8) for dev in range(...]
    all_gather x3 -> x0, waiting for transfers between devices: 125 us -> none  [per_device(): gathered = lax.all_gather(average, 'cluster', axis=0, tiled=True)]
    dot_general x3, matrix products: 16.4 us -> 6.74 us  [per_device(): jnp.einsum('rsk,rjk->rsj', rhs, solve_block, preferred_element_type=jnp.f...]
    concatenate x0 -> x5, other arithmetic: none -> 8.42 us  [the longest x2 8.34 us: per_device(): jnp.roll(jnp.concatenate(ring[::-1], axis=0), (lax.axis_index('cluster')...]
    unnamed x10 -> x59, local copies, waits for them, and re-layouts: 0.02 us -> 7.14 us
  transfers between devices with their start and end apart: 6 -> 24, of which waited for: 6 -> 24; matrix products, arithmetic and copies ran while one was open for 0% -> 0% of each run, Pallas kernels for 0% -> 0%
where the time goes in v1:
time: 450 us
  waiting for transfers between devices  390 us (87%)
  other arithmetic  19.4 us (4%)
  between operations  13.6 us (3%)
  local copies, waits for them, and re-layouts  9.52 us (2%)
  matrix products  8.77 us (2%)
  blocking collectives  5.67 us (1%)
    reduce_scatter x3, waiting for transfers between devices, per_device(): share = lax.psum_scatter(flat, 'cluster', scatter_dimension=0, tiled=True)  213 us
    ppermute x21, waiting for transfers between devices, per_device(): lax.ppermute(ring[-1], 'cluster', [(dev, (dev + 1) % 8) for dev in range(...  177 us
  transfers between devices with their start and end apart: 24, of which 24 were waited for; matrix products, arithmetic and copies ran while one was open for 0% of the time, Pallas kernels for 0%

profile of v1, /device:TPU:0, one launch (start us, length us, event | category | flops | bytes accessed | tf_op | source)
XLA Modules:
  0.0 449.7 jit_solution(15307624189901975374)
XLA Ops:
  6.5 1.1 fusion.32
  7.6 0.0 copy-start.18
  7.6 1.1 slice_bitcast_fusion.2
  8.7 1.9 fusion.33
  10.6 1.0 slice_bitcast_fusion
  11.7 0.1 copy.15
  11.8 0.1 broadcast_in_dim.4
  11.9 0.1 mul.33
  12.0 0.0 copy-start.9
  12.0 2.0 fusion.19
  14.1 2.4 fusion.17
  16.5 0.0 reduce-scatter.4.cloned.1.call-update
  16.5 0.0 reduce-scatter.6.cloned.1.call-start
  16.5 74.6 %reduce-scatter.4.cloned.1.call-done = f32[336,256]{1,0:T(8,128)} async-done(((f32[2688,256]{1,0:T(8,128)}), f32[336,256]{1,0:T(8,128)}) %reduce-scatter.4.cloned.1.call-update) | async-done | bytes 344080 | tf_op jit(solution)/shard_map/reduce_scatter | solution.py:34
  91.1 1.1 multiply_convert_fusion.3
  92.2 1.0 collective-permute-start
  93.2 7.1 %collective-permute-done = bf16[336,256]{1,0:T(8,128)(2,1)S(1)} collective-permute-done((bf16[336,256]{1,0:T(8,128)(2,1)S(1)}, bf16[336,256]{1,0:T(8,128)(2,1)S(1)}, u32[]{:S(2)}, u32[]{:S(2)}) %collective-permute-start) | collective-permute-done | bytes 172064 | tf_op jit(solution)/shard_map/ppermute | solution.py:39
  100.3 8.1 %collective-permute-done.1 = bf16[336,256]{1,0:T(8,128)(2,1)S(1)} collective-permute-done((bf16[336,256]{1,0:T(8,128)(2,1)S(1)}, bf16[336,256]{1,0:T(8,128)(2,1)S(1)}, u32[]{:S(2)}, u32[]{:S(2)}) %collective-permute-start.1) | collective-permute-done | bytes 172064 | tf_op jit(solution)/shard_map/ppermute | solution.py:39
  108.4 8.1 %collective-permute-done.2 = bf16[336,256]{1,0:T(8,128)(2,1)S(1)} collective-permute-done((bf16[336,256]{1,0:T(8,128)(2,1)S(1)}, bf16[336,256]{1,0:T(8,128)(2,1)S(1)}, u32[]{:S(2)}, u32[]{:S(2)}) %collective-permute-start.2) | collective-permute-done | bytes 172064 | tf_op jit(solution)/shard_map/ppermute | solution.py:39
  116.5 0.7 copy-done.15
  117.2 8.2 %collective-permute-done.3 = bf16[336,256]{1,0:T(8,128)(2,1)S(1)} collective-permute-done((bf16[336,256]{1,0:T(8,128)(2,1)S(1)}, bf16[336,256]{1,0:T(8,128)(2,1)S(1)}, u32[]{:S(2)}, u32[]{:S(2)}) %collective-permute-start.3) | collective-permute-done | bytes 172064 | tf_op jit(solution)/shard_map/ppermute | solution.py:39
  125.4 0.7 copy-done.16
  126.1 9.4 %collective-permute-done.4 = bf16[336,256]{1,0:T(8,128)(2,1)S(1)} collective-permute-done((bf16[336,256]{1,0:T(8,128)(2,1)S(1)}, bf16[336,256]{1,0:T(8,128)(2,1)S(1)}, u32[]{:S(2)}, u32[]{:S(2)}) %collective-permute-start.4) | collective-permute-done | bytes 172064 | tf_op jit(solution)/shard_map/ppermute | solution.py:39
  135.5 0.7 copy-done.17
  136.1 9.1 %collective-permute-done.5 = bf16[336,256]{1,0:T(8,128)(2,1)} collective-permute-done((bf16[336,256]{1,0:T(8,128)(2,1)S(1)}, bf16[336,256]{1,0:T(8,128)(2,1)}, u32[]{:S(2)}, u32[]{:S(2)}) %collective-permute-start.5) | collective-permute-done | bytes 172064 | tf_op jit(solution)/shard_map/ppermute | solution.py:39
  145.3 8.4 %collective-permute-done.6 = bf16[336,256]{1,0:T(8,128)(2,1)} collective-permute-done((bf16[336,256]{1,0:T(8,128)(2,1)}, bf16[336,256]{1,0:T(8,128)(2,1)}, u32[]{:S(2)}, u32[]{:S(2)}) %collective-permute-start.6) | collective-permute-done | bytes 172064 | tf_op jit(solution)/shard_map/ppermute | solution.py:39
  153.7 0.9 constant_dynamic-update-slice_fusion.7
  154.6 0.9 constant_dynamic-update-slice_fusion.6
  155.5 0.9 constant_dynamic-update-slice_fusion.5
  156.5 1.0 constant_dynamic-update-slice_fusion.4
  157.5 0.0 copy-start.10
  157.5 1.1 constant_dynamic-update-slice_fusion.3
  158.7 4.2 fusion.11
  162.9 2.2 fusion.6
  165.1 0.0 reduce-scatter.6.cloned.1.call-update
  165.1 0.0 reduce-scatter.8.cloned.1.call-start
  165.2 69.0 %reduce-scatter.6.cloned.1.call-done = f32[336,256]{1,0:T(8,128)} async-done(((f32[2688,256]{1,0:T(8,128)}), f32[336,256]{1,0:T(8,128)}) %reduce-scatter.6.cloned.1.call-update) | async-done | bytes 344080 | tf_op jit(solution)/shard_map/reduce_scatter | solution.py:34
  234.2 1.1 multiply_convert_fusion.2
  235.3 1.1 collective-permute-start.7
  236.3 7.1 %collective-permute-done.7 = bf16[336,256]{1,0:T(8,128)(2,1)S(1)} collective-permute-done((bf16[336,256]{1,0:T(8,128)(2,1)S(1)}, bf16[336,256]{1,0:T(8,128)(2,1)S(1)}, u32[]{:S(2)}, u32[]{:S(2)}) %collective-permute-start.7) | collective-permute-done | bytes 172064 | tf_op jit(solution)/shard_map/ppermute | solution.py:39
  243.4 8.1 %collective-permute-done.8 = bf16[336,256]{1,0:T(8,128)(2,1)S(1)} collective-permute-done((bf16[336,256]{1,0:T(8,128)(2,1)S(1)}, bf16[336,256]{1,0:T(8,128)(2,1)S(1)}, u32[]{:S(2)}, u32[]{:S(2)}) %collective-permute-start.8) | collective-permute-done | bytes 172064 | tf_op jit(solution)/shard_map/ppermute | solution.py:39
  251.5 8.1 %collective-permute-done.9 = bf16[336,256]{1,0:T(8,128)(2,1)S(1)} collective-permute-done((bf16[336,256]{1,0:T(8,128)(2,1)S(1)}, bf16[336,256]{1,0:T(8,128)(2,1)S(1)}, u32[]{:S(2)}, u32[]{:S(2)}) %collective-permute-start.9) | collective-permute-done | bytes 172064 | tf_op jit(solution)/shard_map/ppermute | solution.py:39
  259.6 8.8 %collective-permute-done.10 = bf16[336,256]{1,0:T(8,128)(2,1)S(1)} collective-permute-done((bf16[336,256]{1,0:T(8,128)(2,1)S(1)}, bf16[336,256]{1,0:T(8,128)(2,1)S(1)}, u32[]{:S(2)}, u32[]{:S(2)}) %collective-permute-start.10) | collective-permute-done | bytes 172064 | tf_op jit(solution)/shard_map/ppermute | solution.py:39
  268.5 9.9 %collective-permute-done.11 = bf16[336,256]{1,0:T(8,128)(2,1)S(1)} collective-permute-done((bf16[336,256]{1,0:T(8,128)(2,1)S(1)}, bf16[336,256]{1,0:T(8,128)(2,1)S(1)}, u32[]{:S(2)}, u32[]{:S(2)}) %collective-permute-start.11) | collective-permute-done | bytes 172064 | tf_op jit(solution)/shard_map/ppermute | solution.py:39
  278.4 9.0 %collective-permute-done.12 = bf16[336,256]{1,0:T(8,128)(2,1)S(1)} collective-permute-done((bf16[336,256]{1,0:T(8,128)(2,1)S(1)}, bf16[336,256]{1,0:T(8,128)(2,1)S(1)}, u32[]{:S(2)}, u32[]{:S(2)}) %collective-permute-start.12) | collective-permute-done | bytes 172064 | tf_op jit(solution)/shard_map/ppermute | solution.py:39
  287.4 0.0 collective-permute-start.13
  287.4 8.1 %collective-permute-done.13 = bf16[336,256]{1,0:T(8,128)(2,1)S(1)} collective-permute-done((bf16[336,256]{1,0:T(8,128)(2,1)S(1)}, bf16[336,256]{1,0:T(8,128)(2,1)S(1)}, u32[]{:S(2)}, u32[]{:S(2)}) %collective-permute-start.13) | collective-permute-done | bytes 172064 | tf_op jit(solution)/shard_map/ppermute | solution.py:39
  295.6 0.0 copy-start.11
  295.8 4.2 fusion.10
  300.0 2.2 fusion.7
  302.2 0.0 reduce-scatter.8.cloned.1.call-update
  302.2 69.1 %reduce-scatter.8.cloned.1.call-done = f32[336,256]{1,0:T(8,128)} async-done(((f32[2688,256]{1,0:T(8,128)}), f32[336,256]{1,0:T(8,128)}) %reduce-scatter.8.cloned.1.call-update) | async-done | bytes 344080 | tf_op jit(solution)/shard_map/reduce_scatter | solution.py:34
  371.3 1.1 multiply_convert_fusion.1
  372.4 1.0 collective-permute-start.14
  373.4 7.2 %collective-permute-done.14 = bf16[336,256]{1,0:T(8,128)(2,1)S(1)} collective-permute-done((bf16[336,256]{1,0:T(8,128)(2,1)S(1)}, bf16[336,256]{1,0:T(8,128)(2,1)S(1)}, u32[]{:S(2)}, u32[]{:S(2)}) %collective-permute-start.14) | collective-permute-done | bytes 172064 | tf_op jit(solution)/shard_map/ppermute | solution.py:39
  380.5 8.1 %collective-permute-done.15 = bf16[336,256]{1,0:T(8,128)(2,1)S(1)} collective-permute-done((bf16[336,256]{1,0:T(8,128)(2,1)S(1)}, bf16[336,256]{1,0:T(8,128)(2,1)S(1)}, u32[]{:S(2)}, u32[]{:S(2)}) %collective-permute-start.15) | collective-permute-done | bytes 172064 | tf_op jit(solution)/shard_map/ppermute | solution.py:39
  388.6 8.1 %collective-permute-done.16 = bf16[336,256]{1,0:T(8,128)(2,1)S(1)} collective-permute-done((bf16[336,256]{1,0:T(8,128)(2,1)S(1)}, bf16[336,256]{1,0:T(8,128)(2,1)S(1)}, u32[]{:S(2)}, u32[]{:S(2)}) %collective-permute-start.16) | collective-permute-done | bytes 172064 | tf_op jit(solution)/shard_map/ppermute | solution.py:39
  396.7 8.9 %collective-permute-done.17 = bf16[336,256]{1,0:T(8,128)(2,1)S(1)} collective-permute-done((bf16[336,256]{1,0:T(8,128)(2,1)S(1)}, bf16[336,256]{1,0:T(8,128)(2,1)S(1)}, u32[]{:S(2)}, u32[]{:S(2)}) %collective-permute-start.17) | collective-permute-done | bytes 172064 | tf_op jit(solution)/shard_map/ppermute | solution.py:39
  405.6 9.9 %collective-permute-done.18 = bf16[336,256]{1,0:T(8,128)(2,1)S(1)} collective-permute-done((bf16[336,256]{1,0:T(8,128)(2,1)S(1)}, bf16[336,256]{1,0:T(8,128)(2,1)S(1)}, u32[]{:S(2)}, u32[]{:S(2)}) %collective-permute-start.18) | collective-permute-done | bytes 172064 | tf_op jit(solution)/shard_map/ppermute | solution.py:39
  415.5 9.0 %collective-permute-done.19 = bf16[336,256]{1,0:T(8,128)(2,1)S(1)} collective-permute-done((bf16[336,256]{1,0:T(8,128)(2,1)S(1)}, bf16[336,256]{1,0:T(8,128)(2,1)S(1)}, u32[]{:S(2)}, u32[]{:S(2)}) %collective-permute-start.19) | collective-permute-done | bytes 172064 | tf_op jit(solution)/shard_map/ppermute | solution.py:39
  424.5 8.1 %collective-permute-done.20 = bf16[336,256]{1,0:T(8,128)(2,1)S(1)} collective-permute-done((bf16[336,256]{1,0:T(8,128)(2,1)S(1)}, bf16[336,256]{1,0:T(8,128)(2,1)S(1)}, u32[]{:S(2)}, u32[]{:S(2)}) %collective-permute-start.20) | collective-permute-done | bytes 172064 | tf_op jit(solution)/shard_map/ppermute | solution.py:39
  432.8 3.4 multiply_reduce_fusion
  436.2 5.7 %psum.7 = f32[128]{0:T(128)S(1)} all-reduce(f32[128]{0:T(128)S(1)} %slice_add_fusion), channel_id=1, replica_groups=mesh['cluster'=8,'sub'=4] {'sub'}, use_global_device_ids=true, to_apply=%region_4.6 | all-reduce | flops 128 | bytes 1024 | tf_op jit(solution)/shard_map/psum | solution.py:51
  441.8 1.3 multiply_convert_fusion
  (72 shorter events, 0.4 us)
Async XLA Ops:
  6.5 4.1 copy-start.2
  6.5 84.5 %reduce-scatter.4.cloned.1.call-start = ((), (), s32[]{:S(2)}) async-start(), calls=%async_computation.3 | async-start | bytes 3096576 | tf_op jit(solution)/shard_map/reduce_scatter | solution.py:34
  7.6 4.1 copy-start.18
  12.0 2.1 copy-start.6
  12.0 2.1 copy-start.9
  12.0 2.1 copy-start.12
  16.5 217.7 %reduce-scatter.6.cloned.1.call-start = ((), (), s32[]{:S(2)}) async-start(), calls=%async_computation.4 | async-start | bytes 3096576 | tf_op jit(solution)/shard_map/reduce_scatter | solution.py:34
  91.1 67.6 %copy-start.3 = (f32[336,256]{1,0:T(8,128)S(1)}, f32[336,256]{1,0:T(8,128)}, u32[]{:S(2)}) copy-start(f32[336,256]{1,0:T(8,128)} %reduce-scatter.4.cloned.1.call-done) | copy-start | bytes 1032196
  92.2 8.2 %collective-permute-start = (bf16[336,256]{1,0:T(8,128)(2,1)S(1)}, bf16[336,256]{1,0:T(8,128)(2,1)S(1)}, u32[]{:S(2)}, u32[]{:S(2)}) collective-permute-start(bf16[336,256]{1,0:T(8,128)(2,1)S(1)} %multiply_convert_fusion.3), channel_id=1, source_target_pairs={{0,4},{4,8},{8,12},{12,16},{16,20},{20,24},{24,28},{28,0},{1,5},{5... | collective-permute-start | bytes 516104 | tf_op jit(solution)/shard_map/ppermute | solution.py:39
  100.3 8.1 %collective-permute-start.1 = (bf16[336,256]{1,0:T(8,128)(2,1)S(1)}, bf16[336,256]{1,0:T(8,128)(2,1)S(1)}, u32[]{:S(2)}, u32[]{:S(2)}) collective-permute-start(bf16[336,256]{1,0:T(8,128)(2,1)S(1)} %collective-permute-done), channel_id=1, source_target_pairs={{0,4},{4,8},{8,12},{12,16},{16,20},{20,24},{24,28},{28,0},{1,5},{5... | collective-permute-start | bytes 516104 | tf_op jit(solution)/shard_map/ppermute | solution.py:39
  108.4 8.1 %collective-permute-start.2 = (bf16[336,256]{1,0:T(8,128)(2,1)S(1)}, bf16[336,256]{1,0:T(8,128)(2,1)S(1)}, u32[]{:S(2)}, u32[]{:S(2)}) collective-permute-start(bf16[336,256]{1,0:T(8,128)(2,1)S(1)} %collective-permute-done.1), channel_id=1, source_target_pairs={{0,4},{4,8},{8,12},{12,16},{16,20},{20,24},{24,28},{28,0},{1,5},{5... | collective-permute-start | bytes 516104 | tf_op jit(solution)/shard_map/ppermute | solution.py:39
  116.5 0.7 copy-start.15
  117.2 8.2 %collective-permute-start.3 = (bf16[336,256]{1,0:T(8,128)(2,1)S(1)}, bf16[336,256]{1,0:T(8,128)(2,1)S(1)}, u32[]{:S(2)}, u32[]{:S(2)}) collective-permute-start(bf16[336,256]{1,0:T(8,128)(2,1)S(1)} %collective-permute-done.2), channel_id=1, source_target_pairs={{0,4},{4,8},{8,12},{12,16},{16,20},{20,24},{24,28},{28,0},{1,5},{5... | collective-permute-start | bytes 516104 | tf_op jit(solution)/shard_map/ppermute | solution.py:39
  125.4 0.7 copy-start.16
  126.1 9.4 %collective-permute-start.4 = (bf16[336,256]{1,0:T(8,128)(2,1)S(1)}, bf16[336,256]{1,0:T(8,128)(2,1)S(1)}, u32[]{:S(2)}, u32[]{:S(2)}) collective-permute-start(bf16[336,256]{1,0:T(8,128)(2,1)S(1)} %collective-permute-done.3), channel_id=1, source_target_pairs={{0,4},{4,8},{8,12},{12,16},{16,20},{20,24},{24,28},{28,0},{1,5},{5... | collective-permute-start | bytes 516104 | tf_op jit(solution)/shard_map/ppermute | solution.py:39
  135.5 0.7 copy-start.17
  136.1 9.1 %collective-permute-start.5 = (bf16[336,256]{1,0:T(8,128)(2,1)S(1)}, bf16[336,256]{1,0:T(8,128)(2,1)}, u32[]{:S(2)}, u32[]{:S(2)}) collective-permute-start(bf16[336,256]{1,0:T(8,128)(2,1)S(1)} %collective-permute-done.4), channel_id=1, source_target_pairs={{0,4},{4,8},{8,12},{12,16},{16,20},{20,24},{24,28},{28,0},{1,5},{5... | collective-permute-start | bytes 516104 | tf_op jit(solution)/shard_map/ppermute | solution.py:39
  145.2 8.4 %collective-permute-start.6 = (bf16[336,256]{1,0:T(8,128)(2,1)}, bf16[336,256]{1,0:T(8,128)(2,1)}, u32[]{:S(2)}, u32[]{:S(2)}) collective-permute-start(bf16[336,256]{1,0:T(8,128)(2,1)} %collective-permute-done.5), channel_id=1, source_target_pairs={{0,4},{4,8},{8,12},{12,16},{16,20},{20,24},{24,28},{28,0},{1,5},{5... | collective-permute-start | bytes 516104 | tf_op jit(solution)/shard_map/ppermute | solution.py:39
  156.5 6.4 %copy-start.13 = (bf16[16,128,128]{2,1,0:T(8,128)(2,1)S(1)}, bf16[16,128,128]{2,1,0:T(8,128)(2,1)}, u32[]{:S(2)}) copy-start(bf16[16,128,128]{2,1,0:T(8,128)(2,1)} %get-tuple-element.9) | copy-start | bytes 1572868
  157.5 5.4 %copy-start = (f32[16,168,256]{2,1,0:T(8,128)S(1)}, f32[16,168,256]{2,1,0:T(8,128)}, u32[]{:S(2)}) copy-start(f32[16,168,256]{2,1,0:T(8,128)} %fusion.17) | copy-start | bytes 8257540
  157.5 5.4 %copy-start.7 = (bf16[16,128,128]{2,1,0:T(8,128)(2,1)S(1)}, bf16[16,128,128]{2,1,0:T(8,128)(2,1)}, u32[]{:S(2)}) copy-start(bf16[16,128,128]{2,1,0:T(8,128)(2,1)} %fusion.33) | copy-start | bytes 1572868
  157.5 5.4 %copy-start.10 = (bf16[16,128,128]{2,1,0:T(8,128)(2,1)S(1)}, bf16[16,128,128]{2,1,0:T(8,128)(2,1)}, u32[]{:S(2)}) copy-start(bf16[16,128,128]{2,1,0:T(8,128)(2,1)} %get-tuple-element.8) | copy-start | bytes 1572868
  165.1 206.2 %reduce-scatter.8.cloned.1.call-start = ((), (), s32[]{:S(2)}) async-start(), calls=%async_computation.5 | async-start | bytes 3096576 | tf_op jit(solution)/shard_map/reduce_scatter | solution.py:34
  234.2 61.5 %copy-start.4 = (f32[336,256]{1,0:T(8,128)S(1)}, f32[336,256]{1,0:T(8,128)}, u32[]{:S(2)}) copy-start(f32[336,256]{1,0:T(8,128)} %reduce-scatter.6.cloned.1.call-done) | copy-start | bytes 1032196
  235.3 8.2 %collective-permute-start.7 = (bf16[336,256]{1,0:T(8,128)(2,1)S(1)}, bf16[336,256]{1,0:T(8,128)(2,1)S(1)}, u32[]{:S(2)}, u32[]{:S(2)}) collective-permute-start(bf16[336,256]{1,0:T(8,128)(2,1)S(1)} %multiply_convert_fusion.2), channel_id=1, source_target_pairs={{0,4},{4,8},{8,12},{12,16},{16,20},{20,24},{24,28},{28,0},{1,5},{5... | collective-permute-start | bytes 516104 | tf_op jit(solution)/shard_map/ppermute | solution.py:39
  243.4 8.1 %collective-permute-start.8 = (bf16[336,256]{1,0:T(8,128)(2,1)S(1)}, bf16[336,256]{1,0:T(8,128)(2,1)S(1)}, u32[]{:S(2)}, u32[]{:S(2)}) collective-permute-start(bf16[336,256]{1,0:T(8,128)(2,1)S(1)} %collective-permute-done.7), channel_id=1, source_target_pairs={{0,4},{4,8},{8,12},{12,16},{16,20},{20,24},{24,28},{28,0},{1,5},{5... | collective-permute-start | bytes 516104 | tf_op jit(solution)/shard_map/ppermute | solution.py:39
  251.5 8.1 %collective-permute-start.9 = (bf16[336,256]{1,0:T(8,128)(2,1)S(1)}, bf16[336,256]{1,0:T(8,128)(2,1)S(1)}, u32[]{:S(2)}, u32[]{:S(2)}) collective-permute-start(bf16[336,256]{1,0:T(8,128)(2,1)S(1)} %collective-permute-done.8), channel_id=1, source_target_pairs={{0,4},{4,8},{8,12},{12,16},{16,20},{20,24},{24,28},{28,0},{1,5},{5... | collective-permute-start | bytes 516104 | tf_op jit(solution)/shard_map/ppermute | solution.py:39
  259.6 8.8 %collective-permute-start.10 = (bf16[336,256]{1,0:T(8,128)(2,1)S(1)}, bf16[336,256]{1,0:T(8,128)(2,1)S(1)}, u32[]{:S(2)}, u32[]{:S(2)}) collective-permute-start(bf16[336,256]{1,0:T(8,128)(2,1)S(1)} %collective-permute-done.9), channel_id=1, source_target_pairs={{0,4},{4,8},{8,12},{12,16},{16,20},{20,24},{24,28},{28,0},{1,5},{5... | collective-permute-start | bytes 516104 | tf_op jit(solution)/shard_map/ppermute | solution.py:39
  268.5 9.9 %collective-permute-start.11 = (bf16[336,256]{1,0:T(8,128)(2,1)S(1)}, bf16[336,256]{1,0:T(8,128)(2,1)S(1)}, u32[]{:S(2)}, u32[]{:S(2)}) collective-permute-start(bf16[336,256]{1,0:T(8,128)(2,1)S(1)} %collective-permute-done.10), channel_id=1, source_target_pairs={{0,4},{4,8},{8,12},{12,16},{16,20},{20,24},{24,28},{28,0},{1,5},{5... | collective-permute-start | bytes 516104 | tf_op jit(solution)/shard_map/ppermute | solution.py:39
  278.4 9.0 %collective-permute-start.12 = (bf16[336,256]{1,0:T(8,128)(2,1)S(1)}, bf16[336,256]{1,0:T(8,128)(2,1)S(1)}, u32[]{:S(2)}, u32[]{:S(2)}) collective-permute-start(bf16[336,256]{1,0:T(8,128)(2,1)S(1)} %collective-permute-done.11), channel_id=1, source_target_pairs={{0,4},{4,8},{8,12},{12,16},{16,20},{20,24},{24,28},{28,0},{1,5},{5... | collective-permute-start | bytes 516104 | tf_op jit(solution)/shard_map/ppermute | solution.py:39
  287.4 8.1 %collective-permute-start.13 = (bf16[336,256]{1,0:T(8,128)(2,1)S(1)}, bf16[336,256]{1,0:T(8,128)(2,1)S(1)}, u32[]{:S(2)}, u32[]{:S(2)}) collective-permute-start(bf16[336,256]{1,0:T(8,128)(2,1)S(1)} %collective-permute-done.12), channel_id=1, source_target_pairs={{0,4},{4,8},{8,12},{12,16},{16,20},{20,24},{24,28},{28,0},{1,5},{5... | collective-permute-start | bytes 516104 | tf_op jit(solution)/shard_map/ppermute | solution.py:39
  295.6 4.4 copy-start.14
  295.6 4.3 copy-start.1
  295.6 4.3 copy-start.8
  295.6 4.3 copy-start.11
  371.3 61.4 %copy-start.5 = (f32[336,256]{1,0:T(8,128)S(1)}, f32[336,256]{1,0:T(8,128)}, u32[]{:S(2)}) copy-start(f32[336,256]{1,0:T(8,128)} %reduce-scatter.8.cloned.1.call-done) | copy-start | bytes 1032196
  372.4 8.2 %collective-permute-start.14 = (bf16[336,256]{1,0:T(8,128)(2,1)S(1)}, bf16[336,256]{1,0:T(8,128)(2,1)S(1)}, u32[]{:S(2)}, u32[]{:S(2)}) collective-permute-start(bf16[336,256]{1,0:T(8,128)(2,1)S(1)} %multiply_convert_fusion.1), channel_id=1, source_target_pairs={{0,4},{4,8},{8,12},{12,16},{16,20},{20,24},{24,28},{28,0},{1,5},{5... | collective-permute-start | bytes 516104 | tf_op jit(solution)/shard_map/ppermute | solution.py:39
  380.5 8.1 %collective-permute-start.15 = (bf16[336,256]{1,0:T(8,128)(2,1)S(1)}, bf16[336,256]{1,0:T(8,128)(2,1)S(1)}, u32[]{:S(2)}, u32[]{:S(2)}) collective-permute-start(bf16[336,256]{1,0:T(8,128)(2,1)S(1)} %collective-permute-done.14), channel_id=1, source_target_pairs={{0,4},{4,8},{8,12},{12,16},{16,20},{20,24},{24,28},{28,0},{1,5},{5... | collective-permute-start | bytes 516104 | tf_op jit(solution)/shard_map/ppermute | solution.py:39
  388.6 8.1 %collective-permute-start.16 = (bf16[336,256]{1,0:T(8,128)(2,1)S(1)}, bf16[336,256]{1,0:T(8,128)(2,1)S(1)}, u32[]{:S(2)}, u32[]{:S(2)}) collective-permute-start(bf16[336,256]{1,0:T(8,128)(2,1)S(1)} %collective-permute-done.15), channel_id=1, source_target_pairs={{0,4},{4,8},{8,12},{12,16},{16,20},{20,24},{24,28},{28,0},{1,5},{5... | collective-permute-start | bytes 516104 | tf_op jit(solution)/shard_map/ppermute | solution.py:39
  396.7 8.9 %collective-permute-start.17 = (bf16[336,256]{1,0:T(8,128)(2,1)S(1)}, bf16[336,256]{1,0:T(8,128)(2,1)S(1)}, u32[]{:S(2)}, u32[]{:S(2)}) collective-permute-start(bf16[336,256]{1,0:T(8,128)(2,1)S(1)} %collective-permute-done.16), channel_id=1, source_target_pairs={{0,4},{4,8},{8,12},{12,16},{16,20},{20,24},{24,28},{28,0},{1,5},{5... | collective-permute-start | bytes 516104 | tf_op jit(solution)/shard_map/ppermute | solution.py:39
  405.6 9.9 %collective-permute-start.18 = (bf16[336,256]{1,0:T(8,128)(2,1)S(1)}, bf16[336,256]{1,0:T(8,128)(2,1)S(1)}, u32[]{:S(2)}, u32[]{:S(2)}) collective-permute-start(bf16[336,256]{1,0:T(8,128)(2,1)S(1)} %collective-permute-done.17), channel_id=1, source_target_pairs={{0,4},{4,8},{8,12},{12,16},{16,20},{20,24},{24,28},{28,0},{1,5},{5... | collective-permute-start | bytes 516104 | tf_op jit(solution)/shard_map/ppermute | solution.py:39
  415.5 9.0 %collective-permute-start.19 = (bf16[336,256]{1,0:T(8,128)(2,1)S(1)}, bf16[336,256]{1,0:T(8,128)(2,1)S(1)}, u32[]{:S(2)}, u32[]{:S(2)}) collective-permute-start(bf16[336,256]{1,0:T(8,128)(2,1)S(1)} %collective-permute-done.18), channel_id=1, source_target_pairs={{0,4},{4,8},{8,12},{12,16},{16,20},{20,24},{24,28},{28,0},{1,5},{5... | collective-permute-start | bytes 516104 | tf_op jit(solution)/shard_map/ppermute | solution.py:39
  424.5 8.1 %collective-permute-start.20 = (bf16[336,256]{1,0:T(8,128)(2,1)S(1)}, bf16[336,256]{1,0:T(8,128)(2,1)S(1)}, u32[]{:S(2)}, u32[]{:S(2)}) collective-permute-start(bf16[336,256]{1,0:T(8,128)(2,1)S(1)} %collective-permute-done.19), channel_id=1, source_target_pairs={{0,4},{4,8},{8,12},{12,16},{16,20},{20,24},{24,28},{28,0},{1,5},{5... | collective-permute-start | bytes 516104 | tf_op jit(solution)/shard_map/ppermute | solution.py:39
Sparse Core Ops, SparseCore 0:
  16.6 74.4 reduce-scatter.3
  165.2 68.9 reduce-scatter.5
  302.3 68.9 reduce-scatter.7
